TPU v7x, 32 devices: a 4x2x2 block of a 4x4x8 slice. The times are simulated.
32 devices in a mesh: dp: 4 (over y, z), ep: 8 (over x, core).
Axes of the slice: x: 4, y: 2, z: 2, core: 2. Of those that a mesh axis runs over, the one named last changes fastest.
The devices are a block of a 4x4x8 slice.
Arguments:
- hidden: bfloat16 [8192, 2048], P(('dp', 'ep')), parts along dimension 0
- router_w: float32 [2048, 32], replicated
- expert_ids: int32 [8192, 2], P(('dp', 'ep')), parts along dimension 0
- w_gate: bfloat16 [32, 2048, 3072], P('ep')
- w_up: bfloat16 [32, 2048, 3072], P('ep')
- w_down: bfloat16 [32, 3072, 2048], P('ep')
- post_scale: float32 [2], replicated
Outputs:
- output: bfloat16 [8192, 2048], P(('dp', 'ep')), parts along dimension 0
There are 4 independent parts. A program takes and returns all parts, laid end to end along the dimension named above; an argument that names none is the same for every part.
All inputs are finite; a program needn't handle non-finite values.
Results may differ from a plain program's by a relative error of at most 0.001.
Values are sent between devices in bfloat16 or wider.
A program may use at most 768 MiB of HBM per device.

v0:
```python
import jax
import jax.numpy as jnp
from jax import lax
from jax.sharding import PartitionSpec as P


def route_tables(hidden, router_w, expert_ids, experts, capacity):
    tokens, choice_count = expert_ids.shape
    logits = jnp.dot(hidden.astype(jnp.float32), router_w, precision=lax.Precision.HIGHEST, preferred_element_type=jnp.float32)
    router_prob = jax.nn.softmax(logits, axis=-1)
    pick_mask = expert_ids[:, :, None] == jnp.arange(experts, dtype=jnp.int32)[None, None, :]
    picked = jnp.sum(jnp.where(pick_mask, router_prob[:, None, :], 0.0), axis=-1)
    gates = picked / jnp.sum(picked, axis=1, keepdims=True)
    pair_hot = pick_mask.reshape(tokens * choice_count, experts).astype(jnp.int32)
    earlier = jnp.cumsum(pair_hot, axis=0) - pair_hot
    slot_of = jnp.sum(earlier * pair_hot, axis=1).reshape(tokens, choice_count)
    slot_mask = slot_of[:, :, None] == jnp.arange(capacity, dtype=jnp.int32)[None, None, :]
    place = pick_mask[:, :, :, None] & slot_mask[:, :, None, :]
    return gates, place


def solution(mesh):
    ep_size = mesh.shape['ep']

    def local_step(hidden, router_w, expert_ids, w_gate, w_up, w_down, post_scale):
        tokens, model_width = hidden.shape
        local_experts = w_gate.shape[0]
        experts = local_experts * ep_size
        capacity = tokens // max(1, experts // 8)
        gates, place = route_tables(hidden, router_w, expert_ids, experts, capacity)
        token_table = jnp.any(place, axis=1).astype(jnp.bfloat16)
        outgoing = jnp.einsum('tec,td->ecd', token_table, hidden, preferred_element_type=jnp.float32).astype(jnp.bfloat16)
        incoming = lax.all_to_all(outgoing, 'ep', 0, 0, tiled=True).reshape(ep_size, local_experts, capacity, model_width)
        gate_in = jnp.einsum('slcd,ldf->slcf', incoming, w_gate, preferred_element_type=jnp.float32)
        up_in = jnp.einsum('slcd,ldf->slcf', incoming, w_up, preferred_element_type=jnp.float32)
        middle = (jax.nn.silu(gate_in) * up_in).astype(jnp.bfloat16)
        expert_out = jnp.einsum('slcf,lfd->slcd', middle, w_down, preferred_element_type=jnp.float32).astype(jnp.bfloat16)
        returned = lax.all_to_all(expert_out.reshape(experts, capacity, model_width), 'ep', 0, 0, tiled=True)
        pair_out = jnp.einsum('tkec,ecd->tkd', place.astype(jnp.bfloat16), returned, preferred_element_type=jnp.float32)
        mixed = jnp.sum(gates[:, :, None] * pair_out, axis=1)
        result = post_scale[0] * hidden.astype(jnp.float32) + post_scale[1] * mixed
        return result.astype(jnp.bfloat16)

    tok_spec = P(('dp', 'ep'))
    return jax.shard_map(local_step, mesh=mesh, in_specs=(tok_spec, P(), tok_spec, P('ep'), P('ep'), P('ep'), P()), out_specs=tok_spec, check_vma=False)
```

profile of v0, /device:TPU:81, one launch (start us, length us, event | category | flops | bytes accessed | tf_op | source)
XLA Modules:
  0.0 343.2 jit_solution(7144600542003279910)
XLA Ops:
  0.0 0.9 copy.9
  0.9 0.1 eq.58
  1.0 0.1 eq.62
  1.2 0.7 iota_compare_fusion.3
  1.9 1.2 reduce-window.6
  3.0 0.2 slice_reduce_fusion
  3.3 0.1 fusion.31
  3.4 0.1 eq.66
  3.6 0.1 copy.12
  3.7 0.0 copy-start.2
  3.7 0.6 copy-done.2
  4.3 0.5 and_reduce_fusion
  4.8 3.6 %convolution_convert_fusion = bf16[32,64,2048]{2,1,0:T(8,128)(2,1)S(1)} fusion(pred[256,32,64]{0,2,1:T(8,128)(4,1)S(1)} %and_reduce_fusion, bf16[256,2048]{1,0:T(8,128)(2,1)} %param.7), kind=kOutput, calls=%fused_computation.19 | convolution fusion | flops 2151677952 | bytes 9961472 | tf_op jit(solution)/shard_map/tec,td->ecd/dot_general | solution.py:32
  8.4 99.4 %all_to_all.10 = bf16[32,64,2048]{2,1,0:T(8,128)(2,1)} all-to-all(bf16[32,64,2048]{2,1,0:T(8,128)(2,1)S(1)} %convolution_convert_fusion), channel_id=1, replica_groups=mesh['dp'=4,'ep'=8] {'ep'}, dimensions={0} | all-to-all | bytes 16777216 | tf_op jit(solution)/shard_map/all_to_all | solution.py:33
  107.8 37.7 %fusion.2 = f32[4,8,64,3072]{3,2,1,0:T(8,128)} fusion(bf16[4,2048,3072]{2,1,0:T(8,128)(2,1)} %param.11, bf16[8,4,64,2048]{3,2,1,0:T(8,128)(2,1)} %bitcast.88), kind=kOutput, calls=%fused_computation.2 | convolution fusion | flops 25769803776 | bytes 83886080 | tf_op jit(solution)/shard_map/slcd,ldf->slcf/dot_general | solution.py:35
  145.5 37.7 %fusion.4 = f32[4,8,64,3072]{3,2,1,0:T(8,128)} fusion(bf16[4,2048,3072]{2,1,0:T(8,128)(2,1)} %param.10, bf16[8,4,64,2048]{3,2,1,0:T(8,128)(2,1)} %bitcast.89), kind=kOutput, calls=%fused_computation.4 | convolution fusion | flops 25769803776 | bytes 83886080 | tf_op jit(solution)/shard_map/slcd,ldf->slcf/dot_general | solution.py:34
  183.2 41.1 %convert_bitcast_fusion = bf16[8,4,64,2048]{3,2,0,1:T(8,128)(2,1)} fusion(bf16[4,3072,2048]{2,1,0:T(8,128)(2,1)} %param.12, f32[4,8,64,3072]{3,2,1,0:T(8,128)} %fusion.2, f32[4,8,64,3072]{3,2,1,0:T(8,128)} %fusion.4), kind=kOutput, calls=%fused_computation.16 | convolution fusion | flops 25811746816 | bytes 109051904 | tf_op jit(solution)/shard_map/slcf,lfd->slcd/dot_general | solution.py:37
  224.3 8.3 %copy.14 = bf16[8,4,64,2048]{3,2,1,0:T(8,128)(2,1)} copy(bf16[8,4,64,2048]{3,2,0,1:T(8,128)(2,1)} %convert_bitcast_fusion) | data formatting | bytes 16777216 | tf_op jit(solution)/shard_map/convert_element_type | solution.py:37
  232.6 6.1 %all-to-all-start.1 = ((bf16[32,64,2048]{2,1,0:T(8,128)(2,1)}), bf16[32,64,2048]{2,1,0:T(8,128)(2,1)}, u32[]{:S(2)}, u32[]{:S(2)}) async-start(bf16[32,64,2048]{2,1,0:T(8,128)(2,1)} %bitcast.87), calls=%async_computation.1 | async-start | bytes 16777216 | tf_op jit(solution)/shard_map/all_to_all | solution.py:38
  238.7 0.7 fusion.36
  239.4 1.0 fusion.37
  240.5 91.8 %all-to-all-done.1 = bf16[32,64,2048]{2,1,0:T(8,128)(2,1)} async-done(((bf16[32,64,2048]{2,1,0:T(8,128)(2,1)}), bf16[32,64,2048]{2,1,0:T(8,128)(2,1)}, u32[]{:S(2)}, u32[]{:S(2)}) %all-to-all-start.1) | async-done | bytes 8388640 | tf_op jit(solution)/shard_map/all_to_all | solution.py:38
  332.3 8.4 %fusion.21 = f32[256,2048]{1,0:T(8,128)S(1)} fusion(bf16[32,64,2048]{2,1,0:T(8,128)(2,1)} %all-to-all-done.1, f32[256,2]{0,1:T(2,128)S(1)} %broadcast_divide_fusion, pred[256,2,64]{0,2,1:T(8,128)(4,1)S(1)} %copy-done.3, pred[256,2,32]{0,2,1:T(8,128)(4,1)S(1)} %copy-done.5), kind=kOutput, calls=%fused_computation.23 | convolution fusion | flops 4297588736 | bytes 10536960 | tf_op jit(solution)/shard_map/tkec,ecd->tkd/dot_general | solution.py:39
  340.7 2.6 add_convert_fusion
  (22 shorter events, 0.2 us)
Async XLA Ops:
  0.0 239.4 %copy-start = (f32[2048,32]{0,1:T(8,128)S(1)}, f32[2048,32]{0,1:T(8,128)}, u32[]{:S(2)}) copy-start(f32[2048,32]{0,1:T(8,128)} %param.8) | copy-start | bytes 786436
  1.9 106.0 %copy-start.4 = (pred[256,2,32]{0,2,1:T(8,128)(4,1)}, pred[256,2,32]{0,2,1:T(8,128)(4,1)S(1)}, u32[]{:S(2)}) copy-start(pred[256,2,32]{0,2,1:T(8,128)(4,1)S(1)} %iota_compare_fusion.3) | copy-start | bytes 49156
  3.7 0.6 copy-start.2
  232.5 6.2 %copy-start.7 = (f32[2]{0:T(128)S(1)}, f32[2]{0:T(128)}, u32[]{:S(2)}) copy-start(f32[2]{0:T(128)} %param.13) | copy-start | bytes 28
  232.5 6.8 %copy-start.1 = (bf16[256,2048]{1,0:T(8,128)(2,1)S(1)}, bf16[256,2048]{1,0:T(8,128)(2,1)}, u32[]{:S(2)}) copy-start(bf16[256,2048]{1,0:T(8,128)(2,1)} %param.7) | copy-start | bytes 3145732
  232.5 7.9 %copy-start.6 = (s32[256,2]{0,1:T(2,128)S(1)}, s32[256,2]{0,1:T(2,128)}, u32[]{:S(2)}) copy-start(s32[256,2]{0,1:T(2,128)} %param.9) | copy-start | bytes 6148
  232.5 99.8 %copy-start.3 = (pred[256,2,64]{0,2,1:T(8,128)(4,1)S(1)}, pred[256,2,64]{0,2,1:T(8,128)(4,1)}, u32[]{:S(2)}) copy-start(pred[256,2,64]{0,2,1:T(8,128)(4,1)} %copy-done.2) | copy-start | bytes 98308
  232.5 99.8 %copy-start.5 = (pred[256,2,32]{0,2,1:T(8,128)(4,1)S(1)}, pred[256,2,32]{0,2,1:T(8,128)(4,1)}, u32[]{:S(2)}) copy-start(pred[256,2,32]{0,2,1:T(8,128)(4,1)} %copy-done.4) | copy-start | bytes 49156
  232.6 99.7 %all-to-all-start.1 = ((bf16[32,64,2048]{2,1,0:T(8,128)(2,1)}), bf16[32,64,2048]{2,1,0:T(8,128)(2,1)}, u32[]{:S(2)}, u32[]{:S(2)}) async-start(bf16[32,64,2048]{2,1,0:T(8,128)(2,1)} %bitcast.87), calls=%async_computation.1 | async-start | bytes 16777216 | tf_op jit(solution)/shard_map/all_to_all | solution.py:38
where the time goes:
time: 344 us; the launch traced here: 343 us
  matrix products  129 us (38%)
  blocking collectives  99.4 us (29%)
  waiting for transfers between devices  91.8 us (27%)
  local copies, waits for them, and re-layouts  11.1 us (3%)
  starting transfers between devices  6.13 us (2%)
  other arithmetic  5.21 us (2%)
    all_to_all x1, blocking collectives, local_step(): lax.all_to_all(outgoing, 'ep', 0, 0, tiled=True)  99.4 us
    all_to_all x1, waiting for transfers between devices, local_step(): lax.all_to_all(expert_out.reshape(experts, capacity, model_width), 'ep',...  91.8 us
    dot_general x1, matrix products, local_step(): jnp.einsum('slcf,lfd->slcd', middle, w_down, preferred_element_type=jnp.f...  41.1 us
    dot_general x1, matrix products, local_step(): jnp.einsum('slcd,ldf->slcf', incoming, w_gate, preferred_element_type=jnp...  37.7 us
    dot_general x1, matrix products, local_step(): jnp.einsum('slcd,ldf->slcf', incoming, w_up, preferred_element_type=jnp.f...  37.7 us
    dot_general x1, matrix products, local_step(): jnp.einsum('tkec,ecd->tkd', place.astype(jnp.bfloat16), returned, preferr...  8.36 us
    convert_element_type x1, local copies, waits for them, and re-layouts, local_step(): jnp.einsum('slcf,lfd->slcd', middle, w_down, preferred_element_type=jnp.f...  8.25 us
  transfers between devices with their start and end apart: 1, of which 1 were waited for; matrix products, arithmetic and copies ran while one was open for 1% of the time, Pallas kernels for 0%

commit v1 on v0

v1 whole, which is shorter than its diff:
```python
import functools

import jax
import jax.numpy as jnp
from jax import lax
from jax.experimental import pallas as pl
from jax.experimental.pallas import tpu as pltpu
from jax.sharding import PartitionSpec as P

MESH = pl.DeviceIdType.MESH
PIECES = 4
TILE = 128
GRAN = 16
F32 = jnp.float32
BF16 = jnp.bfloat16


def dispatch_kernel(n, le, cap, h_ref, wrt_ref, idst_ref, xs_ref, qmap_ref, meta_ref, comb_ref,
                    all_h, all_ids, x_buf, send_sem, ring_sem, pair_sem, x_sem, ids_send, ids_recv):
    ep = lax.axis_index("ep")
    chips = n // 2
    x, c = ep // 2, ep % 2

    def dev(xx, cc):
        return lax.rem(xx + 2 * chips, chips) * 2 + cc

    xp, xm, pa = dev(x + 1, c), dev(x - 1, c), dev(x, 1 - c)
    bar = pltpu.get_barrier_semaphore()
    for o in range(1, n):
        pl.semaphore_signal(bar, inc=1, device_id={"ep": lax.rem(ep + o, n)}, device_id_type=MESH)
    pl.semaphore_wait(bar, n - 1)

    tokens, _ = h_ref.shape
    rows = tokens // PIECES
    started = []

    for o in range(1, n):
        cp = pltpu.make_async_remote_copy(
            src_ref=idst_ref, dst_ref=all_ids.at[ep], send_sem=ids_send.at[o], recv_sem=ids_recv.at[o],
            device_id={"ep": lax.rem(ep + o, n)}, device_id_type=MESH)
        cp.start()
        started.append(cp)
    own_ids = pltpu.make_async_copy(idst_ref, all_ids.at[ep], ids_recv.at[0])
    own_ids.start()

    count = [0]

    def push(src, blk, p, to, rsem):
        cp = pltpu.make_async_remote_copy(
            src_ref=src, dst_ref=all_h.at[blk, pl.ds(p * rows, rows)], send_sem=send_sem.at[count[0]], recv_sem=rsem,
            device_id={"ep": to}, device_id_type=MESH)
        count[0] += 1
        cp.start()
        started.append(cp)

    def arrive(blk, p, sem):
        ref = all_h.at[blk, pl.ds(p * rows, rows)]
        pltpu.make_async_remote_copy(src_ref=ref, dst_ref=ref, send_sem=send_sem.at[0], recv_sem=sem,
                                     device_id={"ep": pa}, device_id_type=MESH).wait_recv()

    last = PIECES - 1
    for s in range(PIECES):
        push(h_ref.at[pl.ds(s * rows, rows)], ep, s, xp, ring_sem.at[0, s])
        push(h_ref.at[pl.ds((last - s) * rows, rows)], ep, last - s, xm, ring_sem.at[1, last - s])
    for s in range(PIECES):
        push(h_ref.at[pl.ds(s * rows, rows)], ep, s, pa, pair_sem.at[0, s])

    own_ids.wait()
    for o in range(1, n):
        ref = all_ids.at[lax.rem(ep + n - o, n)]
        pltpu.make_async_remote_copy(src_ref=ref, dst_ref=ref, send_sem=ids_send.at[o], recv_sem=ids_recv.at[o],
                                     device_id={"ep": pa}, device_id_type=MESH).wait_recv()
    ids0 = all_ids[:, 0, :]
    ids1 = all_ids[:, 1, :]
    experts = n * le
    upper = (lax.broadcasted_iota(jnp.int32, (tokens, tokens), 0)
             < lax.broadcasted_iota(jnp.int32, (tokens, tokens), 1)).astype(F32).astype(BF16)

    def hits(lo, hi):
        return (jnp.where((ids0 >= lo) & (ids0 < hi), 1.0, 0.0) + jnp.where((ids1 >= lo) & (ids1 < hi), 1.0, 0.0))

    lane = lax.broadcasted_iota(jnp.int32, (n, le * cap), 1)
    lane_m = lax.broadcasted_iota(jnp.int32, meta_ref.shape, 1)
    qmap = jnp.full((n, le * cap), -1.0, F32)
    meta = jnp.zeros(meta_ref.shape, F32)
    offset = jnp.where(c > 0, 1.0, 0.0) * jnp.sum(hits(x * 2 * le, x * 2 * le + le), axis=1, keepdims=True)
    slots = []
    for l in range(le):
        e = ep * le + l
        mask = jnp.where((ids0 == e) | (ids1 == e), 1.0, 0.0)
        rank = jnp.dot(mask.astype(BF16), upper, preferred_element_type=F32)
        slots.append(jnp.where(mask > 0.5, rank, -1.0).astype(jnp.int32))
        cnt = jnp.sum(mask, axis=1, keepdims=True)
        inside = lane - l * cap
        insidef = inside.astype(F32)
        qmap = jnp.where((inside >= 0) & (inside < cap) & (insidef < cnt), offset + insidef, qmap)
        meta = jnp.where(lane_m == l, cnt, meta)
        offset = offset + cnt
    qmap_ref[...] = qmap.astype(jnp.int32)
    worst = jnp.zeros((n, 1), F32)
    for j in range(chips):
        worst = jnp.maximum(worst, jnp.sum(hits(j * 2 * le, (j + 1) * 2 * le), axis=1, keepdims=True))
    worst = jnp.max(worst, axis=0, keepdims=True)
    meta_ref[...] = jnp.where(lane_m == le, worst, meta).astype(jnp.int32)

    own0, own1 = idst_ref[0:1, :], idst_ref[1:2, :]
    sub = lax.broadcasted_iota(jnp.int32, (experts, tokens), 0)
    logits = lax.dot_general(wrt_ref[...], h_ref[...].astype(F32), (((1,), (1,)), ((), ())),
                             precision=lax.Precision.HIGHEST, preferred_element_type=F32)
    ex = jnp.exp(logits - jnp.max(logits, axis=0, keepdims=True))
    prob = ex / jnp.sum(ex, axis=0, keepdims=True)
    pick0, pick1 = sub == own0, sub == own1
    p0 = jnp.sum(jnp.where(pick0, prob, 0.0), axis=0, keepdims=True)
    p1 = jnp.sum(jnp.where(pick1, prob, 0.0), axis=0, keepdims=True)
    hot = jnp.where(pick0 | pick1, 1.0, 0.0)
    rank = jnp.dot(hot.astype(BF16), upper, preferred_element_type=F32)
    ei = lax.broadcasted_iota(jnp.int32, (experts, experts), 0)
    ej = lax.broadcasted_iota(jnp.int32, (experts, experts), 1)
    before = ((ei // (2 * le) == ej // (2 * le)) & (ej < ei)).astype(F32).astype(BF16)
    total = jnp.broadcast_to(jnp.sum(hot, axis=1, keepdims=True), (experts, 128)).astype(BF16)
    base = jnp.dot(before, total, preferred_element_type=F32)[:, 0:1]
    where = rank + base
    pos0 = jnp.sum(jnp.where(pick0, where, 0.0), axis=0, keepdims=True)
    pos1 = jnp.sum(jnp.where(pick1, where, 0.0), axis=0, keepdims=True)
    chip0, chip1 = (own0 // (2 * le)).astype(F32), (own1 // (2 * le)).astype(F32)
    row = lax.broadcasted_iota(jnp.int32, (128, tokens), 0)
    packed = jnp.zeros((128, tokens), F32)
    for k, v in enumerate((pos0, pos1, p0 / (p0 + p1), p1 / (p0 + p1), chip0, chip1)):
        packed = jnp.where(row == k, v, packed)
    comb_ref[...] = packed.T

    slot_row = lax.broadcasted_iota(jnp.int32, (cap, tokens), 0)
    moves = []

    def place(i, k):
        all_slots = []
        for l in range(le):
            one = slots[l]
            pick = jnp.sum(jnp.where(lax.broadcasted_iota(jnp.int32, one.shape, 0) == i, one, 0), axis=0, keepdims=True)
            all_slots.append((pick == slot_row).astype(F32).astype(BF16))
        rows_hot = jnp.concatenate(all_slots, axis=0)
        src = h_ref if k == 0 else all_h.at[i]
        half = x_buf.shape[2] // 2
        for q in range(2):
            cols = pl.ds(q * half, half)
            x_buf[k % 2, :, cols] = jnp.dot(rows_hot, src[:, cols], preferred_element_type=F32).astype(BF16)
        for l in range(le):
            cp = pltpu.make_async_copy(x_buf.at[k % 2, pl.ds(l * cap, cap)], xs_ref.at[l, i], x_sem.at[k, l])
            cp.start()
            moves.append(cp)

    def drain(k):
        for cp in moves[k * le:(k + 1) * le]:
            cp.wait()

    place(ep, 0)

    bm, bp, b2 = dev(x - 1, c), dev(x + 1, c), dev(x + 2, c)
    for s in range(PIECES):
        q = last - s
        arrive(bm, s, ring_sem.at[0, s])
        ref = all_h.at[bm, pl.ds(s * rows, rows)]
        if s < PIECES // 2:
            push(ref, bm, s, xp, ring_sem.at[2, s])
        push(ref, bm, s, pa, pair_sem.at[1, s])
        arrive(bp, q, ring_sem.at[1, q])
        ref = all_h.at[bp, pl.ds(q * rows, rows)]
        if s < PIECES // 2:
            push(ref, bp, q, xm, ring_sem.at[2, q])
        push(ref, bp, q, pa, pair_sem.at[2, q])
    for s in range(PIECES // 2):
        for q in (s, last - s):
            arrive(b2, q, ring_sem.at[2, q])
            push(all_h.at[b2, pl.ds(q * rows, rows)], b2, q, pa, pair_sem.at[3, q])
    def landed(i, xx):
        for s in range(PIECES):
            arrive(dev(xx, 1 - c), s, pair_sem.at[i, s])

    landed(0, x)
    place(pa, 1)
    for k, blk in enumerate((bm, bp)):
        drain(k)
        place(blk, 2 + k)
    for k, xx in enumerate((x - 1, x + 1)):
        landed(1 + k, xx)
        drain(2 + k)
        place(dev(xx, 1 - c), 4 + k)
    drain(4)
    place(b2, 6)
    landed(3, x + 2)
    drain(5)
    place(dev(x + 2, 1 - c), 7)
    drain(6)
    drain(7)
    for cp in started:
        cp.wait_send()


def dispatch(n, le, cap, hidden, router_wt, ids_t):
    tokens, width = hidden.shape
    vm = pl.BlockSpec(memory_space=pltpu.VMEM)
    return pl.pallas_call(
        functools.partial(dispatch_kernel, n, le, cap),
        out_shape=(jax.ShapeDtypeStruct((le, n, cap, width), hidden.dtype),
                   jax.ShapeDtypeStruct((n, le * cap), jnp.int32),
                   jax.ShapeDtypeStruct((n, 128), jnp.int32),
                   jax.ShapeDtypeStruct((tokens, 128), F32)),
        in_specs=[vm, vm, vm],
        out_specs=(pl.BlockSpec(memory_space=pl.ANY), vm, vm, vm),
        scratch_shapes=[pltpu.VMEM((n, tokens, width), BF16), pltpu.VMEM((n, 2, tokens), jnp.int32),
                        pltpu.VMEM((2, le * cap, width), BF16), pltpu.SemaphoreType.DMA((PIECES * 7,)),
                        pltpu.SemaphoreType.DMA((3, PIECES)), pltpu.SemaphoreType.DMA((4, PIECES)),
                        pltpu.SemaphoreType.DMA((n, le)), pltpu.SemaphoreType.DMA((n,)),
                        pltpu.SemaphoreType.DMA((n,))],
        compiler_params=pltpu.CompilerParams(collective_id=1, has_side_effects=True,
                                             vmem_limit_bytes=40 * 1024 * 1024),
        name="dispatch",
    )(hidden, router_wt, ids_t)


DEPTH = 4
BLOCK = 512


def experts_kernel(n, le, cap, meta_ref, xs_ref, w1_ref, w3_ref, w2_ref, ys_ref, b1, b3, b2, x_buf, mid, acc, y_buf,
                   w_sem, x_sem, y_sem):
    width, ffn = w1_ref.shape[1:]
    steps = ffn // BLOCK
    total = le * steps

    def weights(s, act):
        l, f, k = s // steps, s % steps, s % DEPTH
        cols = pl.ds(pl.multiple_of(f * BLOCK, BLOCK), BLOCK)
        act(pltpu.make_async_copy(w1_ref.at[l, :, cols], b1.at[k], w_sem.at[k, 0]))
        act(pltpu.make_async_copy(w3_ref.at[l, :, cols], b3.at[k], w_sem.at[k, 1]))
        act(pltpu.make_async_copy(w2_ref.at[l, cols, :], b2.at[k], w_sem.at[k, 2]))

    def count16(i, l):
        return (meta_ref[i, l] + GRAN - 1) // GRAN

    def load_x(l):
        p = l % 2
        at = jnp.int32(0)
        for i in range(n):
            num = count16(i, l)
            for g in range(cap // GRAN):
                @pl.when(g < num)
                def _():
                    pltpu.make_async_copy(xs_ref.at[l, i, pl.ds(g * GRAN, GRAN)],
                                          x_buf.at[p, pl.ds(pl.multiple_of((at + g) * GRAN, GRAN), GRAN)],
                                          x_sem.at[p]).start()
            at = at + num
        x_buf[p, pl.ds(pl.multiple_of(at * GRAN, GRAN), TILE), :] = jnp.zeros((TILE, width), BF16)

    load_x(0)
    for s in range(DEPTH - 1):
        weights(jnp.int32(s), lambda cp: cp.start())

    def put_y(l, act):
        at = jnp.int32(0)
        for i in range(n):
            act(pltpu.make_async_copy(y_buf.at[l % 2, pl.ds(pl.multiple_of(at * GRAN, GRAN), cap)], ys_ref.at[l, i],
                                      y_sem.at[l % 2, i]))
            at = at + count16(i, l)

    def expert(l, carry):
        p = l % 2
        num = jnp.int32(0)
        for i in range(n):
            num = num + count16(i, l)

        def wait_x(_, carry):
            pltpu.make_async_copy(xs_ref.at[0, 0, pl.ds(0, GRAN)], x_buf.at[p, pl.ds(0, GRAN)], x_sem.at[p]).wait()
            return carry

        lax.fori_loop(0, num, wait_x, 0)

        @pl.when(l + 1 < le)
        def _():
            load_x(l + 1)

        @pl.when(l > 1)
        def _():
            put_y(l - 2, lambda cp: cp.wait())

        tiles = (num * GRAN + TILE - 1) // TILE

        def step(f, carry):
            s = l * steps + f
            k = s % DEPTH

            @pl.when(s + DEPTH - 1 < total)
            def _():
                weights(s + DEPTH - 1, lambda cp: cp.start())

            weights(s, lambda cp: cp.wait())

            def rows_of(start, rows):
                sl = pl.ds(pl.multiple_of(start, TILE), rows)
                xt = x_buf[p, sl, :]
                for j in range(BLOCK // 256):
                    cols = pl.ds(j * 256, 256)
                    a = jnp.dot(xt, b1[k, :, cols], preferred_element_type=F32)
                    b = jnp.dot(xt, b3[k, :, cols], preferred_element_type=F32)
                    mid[pl.ds(0, rows), cols] = (a * jax.nn.sigmoid(a) * b).astype(BF16)
                mt = mid[pl.ds(0, rows), :]
                for j in range(width // 512):
                    cols = pl.ds(j * 512, 512)
                    part = jnp.dot(mt, b2[k, :, cols], preferred_element_type=F32)
                    acc[sl, cols] = jnp.where(f == 0, 0.0, acc[sl, cols]) + part

            def pair(r, carry):
                rows_of(r * 2 * TILE, 2 * TILE)
                return carry

            lax.fori_loop(0, tiles // 2, pair, 0)

            @pl.when(tiles % 2 == 1)
            def _():
                rows_of((tiles - 1) * TILE, TILE)

            return carry

        lax.fori_loop(0, steps, step, 0)

        def finish(r, carry):
            sl = pl.ds(pl.multiple_of(r * TILE, TILE), TILE)
            y_buf[p, sl, :] = acc[sl, :].astype(BF16)
            return carry

        lax.fori_loop(0, tiles, finish, 0)
        y_buf[p, pl.ds(pl.multiple_of(tiles * TILE, TILE), cap), :] = jnp.zeros((cap, width), BF16)
        put_y(l, lambda cp: cp.start())
        return carry

    lax.fori_loop(0, le, expert, 0)
    for l in range(max(0, le - 2), le):
        put_y(jnp.int32(l), lambda cp: cp.wait())


def experts(n, le, cap, meta, xs, w_gate, w_up, w_down):
    width, ffn = w_gate.shape[1:]
    full = n * cap
    hbm = pl.BlockSpec(memory_space=pl.ANY)
    return pl.pallas_call(
        functools.partial(experts_kernel, n, le, cap),
        out_shape=jax.ShapeDtypeStruct((le, n, cap, width), BF16),
        in_specs=[pl.BlockSpec(memory_space=pltpu.SMEM), hbm, hbm, hbm, hbm],
        out_specs=hbm,
        scratch_shapes=[pltpu.VMEM((DEPTH, width, BLOCK), BF16), pltpu.VMEM((DEPTH, width, BLOCK), BF16),
                        pltpu.VMEM((DEPTH, BLOCK, width), BF16), pltpu.VMEM((2, full + TILE, width), BF16),
                        pltpu.VMEM((2 * TILE, BLOCK), BF16), pltpu.VMEM((full, width), F32),
                        pltpu.VMEM((2, full + cap, width), BF16), pltpu.SemaphoreType.DMA((DEPTH, 3)),
                        pltpu.SemaphoreType.DMA((2,)), pltpu.SemaphoreType.DMA((2, n))],
        compiler_params=pltpu.CompilerParams(vmem_limit_bytes=60 * 1024 * 1024),
        name="experts",
    )(meta, xs, w_gate, w_up, w_down)


def combine_kernel(n, le, cap, quota, post_ref, qmap_ref, comb_ref, h_ref, ys_ref, out_ref,
                   y_buf, mine, theirs, away, recv_buf, y_sem, pair_send, pair_recv, send_sem, recv_sem):
    ep = lax.axis_index("ep")
    chips = n // 2
    x, c = ep // 2, ep % 2
    pa = x * 2 + 1 - c
    bar = pltpu.get_barrier_semaphore()
    for o in range(1, n):
        pl.semaphore_signal(bar, inc=1, device_id={"ep": lax.rem(ep + o, n)}, device_id_type=MESH)

    order = [(2, 0), (2, 1), (1, 0), (3, 0), (1, 1), (3, 1), (0, 1), (0, 0)]
    dests = [lax.rem(x + dx, chips) * 2 + lax.rem(c + dc, 2) for dx, dc in order]

    def fetch(k):
        return pltpu.make_async_copy(ys_ref.at[:, dests[k]], y_buf.at[k % 2], y_sem.at[k % 2])

    fetch(0).start()
    fetch(1).start()
    pl.semaphore_wait(bar, n - 1)

    tokens, width = h_ref.shape
    row = lax.broadcasted_iota(jnp.int32, (quota, le * cap), 0)
    swaps, copies = [], []

    def pack(k):
        fetch(k).wait()
        slots = qmap_ref[pl.ds(dests[k], 1), :]
        rows = y_buf[k % 2].reshape(le * cap, width)
        away[k] = jnp.dot((slots - (1 - c) * quota == row).astype(F32).astype(BF16), rows,
                          preferred_element_type=F32).astype(BF16)
        cp = pltpu.make_async_remote_copy(src_ref=away.at[k], dst_ref=theirs.at[PARTNER[k]], send_sem=pair_send.at[k],
                                          recv_sem=pair_recv.at[PARTNER[k]], device_id={"ep": pa}, device_id_type=MESH)
        cp.start()
        swaps.append(cp)
        mine[k] = jnp.dot((slots - c * quota == row).astype(F32).astype(BF16), rows,
                          preferred_element_type=F32).astype(BF16)
        if k + 2 < n:
            fetch(k + 2).start()

    def send(k):
        swaps[PARTNER[k]].wait_recv()
        spot = pl.ds(pl.multiple_of(ep * quota, GRAN), quota)
        if k == n - 1:
            recv_buf[spot, :] = mine[k] + theirs[k]
            return
        mine[k] = mine[k] + theirs[k]
        cp = pltpu.make_async_remote_copy(src_ref=mine.at[k], dst_ref=recv_buf.at[spot], send_sem=send_sem.at[k],
                                          recv_sem=recv_sem.at[k], device_id={"ep": dests[k]}, device_id_type=MESH)
        cp.start()
        copies.append(cp)

    PARTNER = [order.index((dx, 1 - dc)) for dx, dc in order]
    pack(0)
    pack(1)
    pack(2)
    send(0)
    send(1)
    for k in range(3, n):
        pack(k)
        if k == 4:
            send(2)
        if k == 5:
            send(3)
            send(4)
    for k in range(5, n):
        send(k)

    pos0, pos1 = comb_ref[:, 0:1], comb_ref[:, 1:2]
    g0, g1 = comb_ref[:, 2:3], comb_ref[:, 3:4]
    pos0 = (comb_ref[:, 4:5] * (2 * quota) + pos0).astype(jnp.int32)
    pos1 = (comb_ref[:, 5:6] * (2 * quota) + pos1).astype(jnp.int32)
    lane = lax.broadcasted_iota(jnp.int32, (tokens, n * quota), 1)
    hot0 = (lane == pos0).astype(F32).astype(BF16)
    hot1 = (lane == pos1).astype(F32).astype(BF16)
    for cp in copies:
        cp.wait()
    for cp in swaps:
        cp.wait_send()
    alpha, beta = post_ref[0], post_ref[1]
    block = 512
    for d in range(width // block):
        cols = pl.ds(d * block, block)
        got = recv_buf[:, cols]
        y0 = jnp.dot(hot0, got, preferred_element_type=F32)
        y1 = jnp.dot(hot1, got, preferred_element_type=F32)
        mixed = g0 * y0 + g1 * y1
        out_ref[:, cols] = (alpha * h_ref[:, cols].astype(F32) + beta * mixed).astype(out_ref.dtype)


def combine(n, le, cap, quota, cid, post_scale, qmap, comb, hidden, ys):
    tokens, width = hidden.shape
    vm = pl.BlockSpec(memory_space=pltpu.VMEM)
    sm = pl.BlockSpec(memory_space=pltpu.SMEM)
    dma = pltpu.SemaphoreType.DMA
    part = pltpu.VMEM((n, quota, width), BF16)
    return pl.pallas_call(
        functools.partial(combine_kernel, n, le, cap, quota),
        out_shape=jax.ShapeDtypeStruct((tokens, width), hidden.dtype),
        in_specs=[sm, vm, vm, vm, pl.BlockSpec(memory_space=pl.ANY)],
        out_specs=vm,
        scratch_shapes=[pltpu.VMEM((2, le, cap, width), BF16), part, part, part,
                        pltpu.VMEM((n * quota, width), BF16), dma((2,)), dma((n,)), dma((n,)), dma((n,)), dma((n,))],
        compiler_params=pltpu.CompilerParams(collective_id=cid, has_side_effects=True,
                                             vmem_limit_bytes=60 * 1024 * 1024),
        name="combine%d" % quota,
    )(post_scale, qmap, comb, hidden, ys)


def solution(mesh):
    n = mesh.shape["ep"]

    def local_step(hidden, router_w, expert_ids, w_gate, w_up, w_down, post_scale):
        tokens, width = hidden.shape
        le = w_gate.shape[0]
        cap = tokens // max(1, (n * le) // 8)
        xs, qmap, meta, comb = dispatch(n, le, cap, hidden, router_w.T, expert_ids.T)
        ys = experts(n, le, cap, meta, xs, w_gate, w_up, w_down)
        quotas = [q for q in (96, 128) if q < le * cap] + [le * cap]
        worst = meta[0, le]
        branch = sum((worst > 2 * q).astype(jnp.int32) for q in quotas[:-1])
        return lax.switch(branch, [functools.partial(combine, n, le, cap, q, 2 + k) for k, q in enumerate(quotas)],
                          post_scale, qmap, comb, hidden, ys)

    tok = P(("dp", "ep"))
    return jax.shard_map(local_step, mesh=mesh, in_specs=(tok, P(), tok, P("ep"), P("ep"), P("ep"), P()),
                         out_specs=tok, check_vma=False)
```

time: 344 us -> 186 us (0.54)
  Pallas kernels: 0 us -> 176 us
  matrix products: 129 us -> 0 us
  blocking collectives: 99.4 us -> 0 us
  waiting for transfers between devices: 91.8 us -> 0 us
  starting transfers between devices: 6.13 us -> 0 us
  other arithmetic: 5.21 us -> 0 us
    pallas_call x0 -> x3, Pallas kernels: none -> 176 us  [the longest x1 78 us: combine(): pl.pallas_call(functools.partial(combine_kernel, n, le, cap, quota), out_...]
    dot_general x6 -> x0, matrix products: 129 us -> none  [the longest x1 41.1 us: local_step(): jnp.einsum('slcf,lfd->slcd', middle, w_down, preferred_element_type=jnp.f...]
    all_to_all x1 -> x0, blocking collectives: 99.4 us -> none  [local_step(): lax.all_to_all(outgoing, 'ep', 0, 0, tiled=True)]
    all_to_all x1 -> x0, waiting for transfers between devices: 91.8 us -> none  [local_step(): lax.all_to_all(expert_out.reshape(experts, capacity, model_width), 'ep',...]
    convert_element_type x1 -> x0, local copies, waits for them, and re-layouts: 8.25 us -> none  [local_step(): jnp.einsum('slcf,lfd->slcd', middle, w_down, preferred_element_type=jnp.f...]
    all_to_all x1 -> x0, starting transfers between devices: 6.13 us -> none  [local_step(): lax.all_to_all(expert_out.reshape(experts, capacity, model_width), 'ep',...]
    unnamed x17 -> x13, local copies, waits for them, and re-layouts: 1.49 us -> 6.44 us
  transfers between devices with their start and end apart: 1 -> 0, of which waited for: 1 -> 0; matrix products, arithmetic and copies ran while one was open for 1% -> 0% of each run, Pallas kernels for 0% -> 0%
where the time goes in v1:
time: 186 us; the launch traced here: 188 us
  Pallas kernels  176 us (95%)
  local copies, waits for them, and re-layouts  7.76 us (4%)
    pallas_call x1, Pallas kernels, combine(): pl.pallas_call(functools.partial(combine_kernel, n, le, cap, quota), out_...  78 us
    pallas_call x1, Pallas kernels, experts(): pl.pallas_call(functools.partial(experts_kernel, n, le, cap), out_shape=j...  51.6 us
    pallas_call x1, Pallas kernels, dispatch(): pl.pallas_call(functools.partial(dispatch_kernel, n, le, cap), out_shape=...  46.8 us
    unnamed x13, local copies, waits for them, and re-layouts  6.44 us

profile of v1, /device:TPU:81, one launch (start us, length us, event | category | flops | bytes accessed | tf_op | source)
XLA Modules:
  0.0 187.6 jit_solution(7255945996355083782)
XLA Ops:
  0.0 0.0 copy-start.1
  0.0 0.9 copy-done.1
  1.0 0.0 copy-start.3
  1.0 0.7 copy-done.3
  1.6 46.8 %dispatch.1 = (bf16[4,8,64,2048]{3,2,1,0:T(8,128)(2,1)S(1)}, s32[8,256]{1,0:T(8,128)S(1)}, s32[8,128]{1,0:T(8,128)S(1)}, f32[256,128]{1,0:T(8,128)S(1)}) custom-call(bf16[256,2048]{1,0:T(8,128)(2,1)} %h_ref.1, f32[32,2048]{1,0:T(8,128)S(1)} %bitcast.3, s32[2,256]{1,0:T(2,128)S(1)} %bitcast.4), custom_call_target="tpu_custom_call" | custom-call | tf_op jit(solution)/shard_map/dispatch/pallas_call | solution.py:202
  48.5 0.0 copy-start
  48.5 3.2 %copy-done = bf16[4,8,64,2048]{3,2,1,0:T(8,128)(2,1)} copy-done((bf16[4,8,64,2048]{3,2,1,0:T(8,128)(2,1)}, bf16[4,8,64,2048]{3,2,1,0:T(8,128)(2,1)S(1)}, u32[]{:S(2)}) %copy-start) | copy-done | bytes 8388632
  51.7 0.0 copy-start.2
  51.7 0.6 copy-done.2
  52.3 0.0 copy-start.4
  52.3 0.0 copy-start.5
  52.3 51.6 %experts.1 = bf16[4,8,64,2048]{3,2,1,0:T(8,128)(2,1)} custom-call(s32[8,128]{1,0:T(8,128)} %copy-done.2, bf16[4,8,64,2048]{3,2,1,0:T(8,128)(2,1)} %copy-done, bf16[4,2048,3072]{2,1,0:T(8,128)(2,1)} %w1_ref.1, bf16[4,2048,3072]{2,1,0:T(8,128)(2,1)} %w3_ref.1, bf16[4,3072,2048]{2,1,0:T(8,128)(2,1)} %w2_ref.1), custom_call_target="tpu_custom_call" | custom-call | tf_op jit(solution)/shard_map/experts/pallas_call | solution.py:345
  104.0 1.3 slice.3
  106.5 0.0 copy-done.4
  106.5 0.0 copy-done.5
  106.6 79.8 %conditional.1 = (bf16[256,2048]{1,0:T(8,128)(2,1)S(1)}) conditional(s32[]{:T(128)} %bitcast.2, (f32[2]{0:T(128)S(1)}, s32[8,256]{1,0:T(8,128)S(1)}, f32[256,128]{1,0:T(8,128)S(1)}, bf16[256,2048]{1,0:T(8,128)(2,1)S(1)}, bf16[4,8,64,2048]{3,2,1,0:T(8,128)(2,1)}) %tuple.24, (f32[2]{0:T(128)S(1)}, s32[8,256]{1,0:T(8,128)S(1)}, ...), branch_computations={%region_0.0_spmd, %region_1.0_spmd, %region_2.0_spmd} | conditional | bytes 8 | solution.py:480
  107.3 78.0 %combine128.1 = bf16[256,2048]{1,0:T(8,128)(2,1)S(1)} custom-call(f32[2]{0:T(128)S(1)} %get-tuple-element.67.post_ref, s32[8,256]{1,0:T(8,128)S(1)} %get-tuple-element.45.qmap_ref, f32[256,128]{1,0:T(8,128)S(1)} %get-tuple-element.46.comb_ref, bf16[256,2048]{1,0:T(8,128)(2,1)S(1)} %get-tuple-element.47.h_ref, bf16[4,8,64,2048]{3,2,1,0:T(8,128)(2,1)} %get-tuple-element.48.ys_ref), custom_call_target="tpu_custom_call" | custom-call | tf_op jit(solution)/shard_map/cond/branch_1_fun/combine128/pallas_call | solution.py:455
  186.4 1.0 copy.18
Async XLA Ops:
  0.0 0.9 copy-start.1
  1.0 0.7 copy-start.3
  48.5 3.2 %copy-start = (bf16[4,8,64,2048]{3,2,1,0:T(8,128)(2,1)}, bf16[4,8,64,2048]{3,2,1,0:T(8,128)(2,1)S(1)}, u32[]{:S(2)}) copy-start(bf16[4,8,64,2048]{3,2,1,0:T(8,128)(2,1)S(1)} %get-tuple-element.61.xs_ref) | copy-start | bytes 25165828
  51.7 0.6 copy-start.2
  52.3 54.2 %copy-start.4 = (bf16[256,2048]{1,0:T(8,128)(2,1)S(1)}, bf16[256,2048]{1,0:T(8,128)(2,1)}, u32[]{:S(2)}) copy-start(bf16[256,2048]{1,0:T(8,128)(2,1)} %h_ref.1) | copy-start | bytes 3145732
  52.3 54.2 %copy-start.5 = (f32[2]{0:T(128)S(1)}, f32[2]{0:T(128)}, u32[]{:S(2)}) copy-start(f32[2]{0:T(128)} %param.16) | copy-start | bytes 28

commit v2 on v1

v2 whole, which is shorter than its diff:
```python
import functools

import jax
import jax.numpy as jnp
from jax import lax
from jax.experimental import pallas as pl
from jax.experimental.pallas import tpu as pltpu
from jax.sharding import PartitionSpec as P

MESH = pl.DeviceIdType.MESH
PIECES = 4
TILE = 128
GRAN = 16
BLOCK = 512
SLOTS = 5
COLS = 256
F32 = jnp.float32
BF16 = jnp.bfloat16


def dispatch_kernel(n, le, cap, h_hbm, wrt_hbm, idst_hbm, w1_ref, w3_ref, xs_ref, qmap_ref, meta_ref,
                    comb_ref, p1_ref, p3_ref, all_h, all_ids, h_ref, wrt_ref, idst_ref, send_sem, ring_sem, pair_sem,
                    in_sem, ids_send, ids_recv, w_sem):
    ep = lax.axis_index("ep")
    chips = n // 2
    x, c = ep // 2, ep % 2

    def dev(xx, cc):
        return lax.rem(xx + 2 * chips, chips) * 2 + cc

    xp, xm, pa = dev(x + 1, c), dev(x - 1, c), dev(x, 1 - c)
    inputs = [pltpu.make_async_copy(src, dst, in_sem.at[k])
              for k, (src, dst) in enumerate(((h_hbm, h_ref), (idst_hbm, idst_ref), (wrt_hbm, wrt_ref)))]
    for cp in inputs:
        cp.start()
    bar = pltpu.get_barrier_semaphore()
    for o in range(1, n):
        pl.semaphore_signal(bar, inc=1, device_id={"ep": lax.rem(ep + o, n)}, device_id_type=MESH)
    tokens, _ = h_ref.shape
    rows = tokens // PIECES
    started, loads = [], []
    inputs[0].wait()
    inputs[1].wait()
    pl.semaphore_wait(bar, n - 1)

    for o in range(1, n):
        cp = pltpu.make_async_remote_copy(
            src_ref=idst_ref, dst_ref=all_ids.at[ep], send_sem=ids_send.at[o], recv_sem=ids_recv.at[o],
            device_id={"ep": lax.rem(ep + o, n)}, device_id_type=MESH)
        cp.start()
        started.append(cp)
    own_ids = pltpu.make_async_copy(idst_ref, all_ids.at[ep], ids_recv.at[0])
    own_ids.start()

    count = [0]

    def push(src, blk, p, to, rsem):
        cp = pltpu.make_async_remote_copy(
            src_ref=src, dst_ref=all_h.at[blk, pl.ds(p * rows, rows)], send_sem=send_sem.at[count[0]], recv_sem=rsem,
            device_id={"ep": to}, device_id_type=MESH)
        count[0] += 1
        cp.start()
        started.append(cp)

    def arrive(blk, p, sem):
        ref = all_h.at[blk, pl.ds(p * rows, rows)]
        pltpu.make_async_remote_copy(src_ref=ref, dst_ref=ref, send_sem=send_sem.at[0], recv_sem=sem,
                                     device_id={"ep": pa}, device_id_type=MESH).wait_recv()

    last = PIECES - 1
    for s in range(PIECES):
        push(h_ref.at[pl.ds(s * rows, rows)], ep, s, xp, ring_sem.at[0, s])
        push(h_ref.at[pl.ds((last - s) * rows, rows)], ep, last - s, xm, ring_sem.at[1, last - s])
    for s in range(PIECES):
        push(h_ref.at[pl.ds(s * rows, rows)], ep, s, pa, pair_sem.at[0, s])

    steps = w1_ref.shape[2] // BLOCK
    for s in range(SLOTS):
        cols = pl.ds(s % steps * BLOCK, BLOCK)
        for k, (src, dst) in enumerate(((w1_ref, p1_ref), (w3_ref, p3_ref))):
            cp = pltpu.make_async_copy(src.at[s // steps, :, cols], dst.at[s], w_sem.at[s, k])
            cp.start()
            loads.append(cp)

    inputs[2].wait()
    own_ids.wait()
    for o in range(1, n):
        ref = all_ids.at[lax.rem(ep + n - o, n)]
        pltpu.make_async_remote_copy(src_ref=ref, dst_ref=ref, send_sem=ids_send.at[o], recv_sem=ids_recv.at[o],
                                     device_id={"ep": pa}, device_id_type=MESH).wait_recv()
    ids0 = all_ids[:, 0, :]
    ids1 = all_ids[:, 1, :]
    experts = n * le
    upper = (lax.broadcasted_iota(jnp.int32, (tokens, tokens), 0)
             < lax.broadcasted_iota(jnp.int32, (tokens, tokens), 1)).astype(F32).astype(BF16)

    def hits(lo, hi):
        return (jnp.where((ids0 >= lo) & (ids0 < hi), 1.0, 0.0) + jnp.where((ids1 >= lo) & (ids1 < hi), 1.0, 0.0))

    lane = lax.broadcasted_iota(jnp.int32, (n, le * cap), 1)
    lane_m = lax.broadcasted_iota(jnp.int32, meta_ref.shape, 1)
    qmap = jnp.full((n, le * cap), -1.0, F32)
    meta = jnp.zeros(meta_ref.shape, F32)
    offset = jnp.where(c > 0, 1.0, 0.0) * jnp.sum(hits(x * 2 * le, x * 2 * le + le), axis=1, keepdims=True)
    slots = []
    for l in range(le):
        e = ep * le + l
        mask = jnp.where((ids0 == e) | (ids1 == e), 1.0, 0.0)
        rank = jnp.dot(mask.astype(BF16), upper, preferred_element_type=F32)
        slots.append(jnp.where(mask > 0.5, rank, -1.0).astype(jnp.int32))
        cnt = jnp.sum(mask, axis=1, keepdims=True)
        inside = lane - l * cap
        insidef = inside.astype(F32)
        qmap = jnp.where((inside >= 0) & (inside < cap) & (insidef < cnt), offset + insidef, qmap)
        meta = jnp.where(lane_m == l, cnt, meta)
        offset = offset + cnt
    qmap_ref[...] = qmap.astype(jnp.int32)
    worst = jnp.zeros((n, 1), F32)
    for j in range(chips):
        worst = jnp.maximum(worst, jnp.sum(hits(j * 2 * le, (j + 1) * 2 * le), axis=1, keepdims=True))
    worst = jnp.max(worst, axis=0, keepdims=True)
    meta_ref[...] = jnp.where(lane_m == le, worst, meta).astype(jnp.int32)

    own0, own1 = idst_ref[0:1, :], idst_ref[1:2, :]
    sub = lax.broadcasted_iota(jnp.int32, (experts, tokens), 0)
    logits = lax.dot_general(wrt_ref[...], h_ref[...].astype(F32), (((1,), (1,)), ((), ())),
                             precision=lax.Precision.HIGHEST, preferred_element_type=F32)
    ex = jnp.exp(logits - jnp.max(logits, axis=0, keepdims=True))
    prob = ex / jnp.sum(ex, axis=0, keepdims=True)
    pick0, pick1 = sub == own0, sub == own1
    p0 = jnp.sum(jnp.where(pick0, prob, 0.0), axis=0, keepdims=True)
    p1 = jnp.sum(jnp.where(pick1, prob, 0.0), axis=0, keepdims=True)
    hot = jnp.where(pick0 | pick1, 1.0, 0.0)
    rank = jnp.dot(hot.astype(BF16), upper, preferred_element_type=F32)
    ei = lax.broadcasted_iota(jnp.int32, (experts, experts), 0)
    ej = lax.broadcasted_iota(jnp.int32, (experts, experts), 1)
    before = ((ei // (2 * le) == ej // (2 * le)) & (ej < ei)).astype(F32).astype(BF16)
    total = jnp.broadcast_to(jnp.sum(hot, axis=1, keepdims=True), (experts, 128)).astype(BF16)
    base = jnp.dot(before, total, preferred_element_type=F32)[:, 0:1]
    where = rank + base
    pos0 = jnp.sum(jnp.where(pick0, where, 0.0), axis=0, keepdims=True)
    pos1 = jnp.sum(jnp.where(pick1, where, 0.0), axis=0, keepdims=True)
    chip0, chip1 = (own0 // (2 * le)).astype(F32), (own1 // (2 * le)).astype(F32)
    row = lax.broadcasted_iota(jnp.int32, (128, tokens), 0)
    packed = jnp.zeros((128, tokens), F32)
    for k, v in enumerate((pos0, pos1, p0 / (p0 + p1), p1 / (p0 + p1), chip0, chip1)):
        packed = jnp.where(row == k, v, packed)
    comb_ref[...] = packed.T

    slot_row = lax.broadcasted_iota(jnp.int32, (cap, tokens), 0)

    def place(i, src):
        one_hot = []
        for l in range(le):
            one = slots[l]
            pick = jnp.sum(jnp.where(lax.broadcasted_iota(jnp.int32, one.shape, 0) == i, one, 0), axis=0, keepdims=True)
            one_hot.append((pick == slot_row).astype(F32).astype(BF16))
        one_hot = jnp.concatenate(one_hot, axis=0)
        half = src.shape[1] // 2
        for q in range(2):
            cols = pl.ds(q * half, half)
            got = jnp.dot(one_hot, src[:, cols], preferred_element_type=F32).astype(BF16)
            for l in range(le):
                xs_ref[l, i, :, cols] = got[l * cap:(l + 1) * cap]

    place(ep, h_ref)

    bm, bp, b2 = dev(x - 1, c), dev(x + 1, c), dev(x + 2, c)
    for s in range(PIECES):
        q = last - s
        arrive(bm, s, ring_sem.at[0, s])
        ref = all_h.at[bm, pl.ds(s * rows, rows)]
        if s < PIECES // 2:
            push(ref, bm, s, xp, ring_sem.at[2, s])
        push(ref, bm, s, pa, pair_sem.at[1, s])
        arrive(bp, q, ring_sem.at[1, q])
        ref = all_h.at[bp, pl.ds(q * rows, rows)]
        if s < PIECES // 2:
            push(ref, bp, q, xm, ring_sem.at[2, q])
        push(ref, bp, q, pa, pair_sem.at[2, q])
    def landed(i, xx):
        for s in range(PIECES):
            arrive(dev(xx, 1 - c), s, pair_sem.at[i, s])

    landed(0, x)
    place(pa, all_h.at[pa])
    place(bm, all_h.at[bm])
    place(bp, all_h.at[bp])
    for k, xx in enumerate((x - 1, x + 1)):
        landed(1 + k, xx)
        place(dev(xx, 1 - c), all_h.at[dev(xx, 1 - c)])
    for r in range(PIECES // 2):
        for q in (r, last - r):
            arrive(b2, q, ring_sem.at[2, q])
            push(all_h.at[b2, pl.ds(q * rows, rows)], b2, q, pa, pair_sem.at[3, q])
    place(b2, all_h.at[b2])
    landed(3, x + 2)
    place(dev(x + 2, 1 - c), all_h.at[dev(x + 2, 1 - c)])
    for cp in started:
        cp.wait_send()
    for cp in loads:
        cp.wait()


def dispatch(n, le, cap, hidden, router_wt, ids_t, w_gate, w_up):
    tokens, width = hidden.shape
    vm = pl.BlockSpec(memory_space=pltpu.VMEM)
    hbm = pl.BlockSpec(memory_space=pltpu.HBM)
    dma = pltpu.SemaphoreType.DMA
    ring = jax.ShapeDtypeStruct((SLOTS, width, BLOCK), BF16)
    return pl.pallas_call(
        functools.partial(dispatch_kernel, n, le, cap),
        out_shape=(jax.ShapeDtypeStruct((le, n, cap, width), hidden.dtype),
                   jax.ShapeDtypeStruct((n, le * cap), jnp.int32),
                   jax.ShapeDtypeStruct((n, 128), jnp.int32),
                   jax.ShapeDtypeStruct((tokens, 128), F32), ring, ring),
        in_specs=[hbm, hbm, hbm, hbm, hbm],
        out_specs=(vm, vm, vm, vm, vm, vm),
        scratch_shapes=[pltpu.VMEM((n, tokens, width), BF16), pltpu.VMEM((n, 2, tokens), jnp.int32),
                        pltpu.VMEM((tokens, width), BF16), pltpu.VMEM(router_wt.shape, F32),
                        pltpu.VMEM(ids_t.shape, jnp.int32), dma((PIECES * 7,)), dma((3, PIECES)), dma((4, PIECES)),
                        dma((3,)), dma((n,)), dma((n,)), dma((SLOTS, 2))],
        compiler_params=pltpu.CompilerParams(collective_id=1, has_side_effects=True,
                                             vmem_limit_bytes=20 * 1024 * 1024),
        name="dispatch",
    )(*[pltpu.with_memory_space_constraint(a, pltpu.HBM) for a in (hidden, router_wt, ids_t, w_gate, w_up)])


def experts_kernel(n, le, cap, meta_ref, xs_ref, w1_ref, w3_ref, _p1, _p3, ms_ref, b1, b3, x_buf, m_buf, w_sem, x_sem,
                   m_sem):
    width, ffn = w1_ref.shape[1:]
    steps = ffn // BLOCK
    total = le * steps
    full = n * cap

    def weights(s, act):
        l, f, k = s // steps, s % steps, s % SLOTS
        cols = pl.ds(pl.multiple_of(f * BLOCK, BLOCK), BLOCK)
        act(pltpu.make_async_copy(w1_ref.at[l, :, cols], b1.at[k], w_sem.at[k, 0]))
        act(pltpu.make_async_copy(w3_ref.at[l, :, cols], b3.at[k], w_sem.at[k, 1]))

    def count16(i, l):
        return (meta_ref[i, l] + GRAN - 1) // GRAN

    def load_x(l):
        p = l % 2
        at = jnp.int32(0)
        for i in range(n):
            num = count16(i, l)
            for g in range(cap // GRAN):
                @pl.when(g < num)
                def _():
                    pltpu.make_async_copy(xs_ref.at[l, i, pl.ds(g * GRAN, GRAN)],
                                          x_buf.at[p, pl.ds(pl.multiple_of((at + g) * GRAN, GRAN), GRAN)],
                                          x_sem.at[p]).start()
            at = at + num
        x_buf[p, pl.ds(pl.multiple_of(at * GRAN, GRAN), TILE), :] = jnp.zeros((TILE, width), BF16)

    load_x(0)

    def put_m(l, act):
        at = jnp.int32(0)
        for i in range(n):
            act(pltpu.make_async_copy(m_buf.at[l % 2, pl.ds(pl.multiple_of(at * GRAN, GRAN), cap)], ms_ref.at[l, pl.ds(i * cap, cap)],
                                      m_sem.at[l % 2, i]))
            at = at + count16(i, l)

    def expert(l, carry):
        p = l % 2
        num = jnp.int32(0)
        for i in range(n):
            num = num + count16(i, l)

        def wait_x(_, carry):
            pltpu.make_async_copy(xs_ref.at[0, 0, pl.ds(0, GRAN)], x_buf.at[p, pl.ds(0, GRAN)], x_sem.at[p]).wait()
            return carry

        lax.fori_loop(0, num, wait_x, 0)

        @pl.when(l + 1 < le)
        def _():
            load_x(l + 1)

        @pl.when(l > 1)
        def _():
            put_m(l - 2, lambda cp: cp.wait())

        tiles = (num * GRAN + TILE - 1) // TILE

        def step(f, carry):
            s = l * steps + f
            k = s % SLOTS

            @pl.when((s > 0) & (s + SLOTS - 1 < total))
            def _():
                weights(s + SLOTS - 1, lambda cp: cp.start())

            @pl.when(s >= SLOTS)
            def _():
                weights(s, lambda cp: cp.wait())

            def rows_of(rows):
                sl = pl.ds(0, rows)
                xt = x_buf[p, sl, :]
                for j in range(BLOCK // 256):
                    cols = pl.ds(j * 256, 256)
                    a = jnp.dot(xt, b1[k, :, cols], preferred_element_type=F32)
                    b = jnp.dot(xt, b3[k, :, cols], preferred_element_type=F32)
                    m_buf[p, sl, pl.ds(pl.multiple_of(f * BLOCK + j * 256, 256), 256)] = (
                        a * jax.nn.sigmoid(a) * b).astype(BF16)

            for t in range(1, full // TILE + 1):
                @pl.when(tiles == t)
                def _():
                    rows_of(t * TILE)

            return carry

        lax.fori_loop(0, steps, step, 0)
        m_buf[p, pl.ds(pl.multiple_of(tiles * TILE, TILE), cap), :] = jnp.zeros((cap, ffn), BF16)
        put_m(l, lambda cp: cp.start())
        return carry

    lax.fori_loop(0, le, expert, 0)
    for l in range(max(0, le - 2), le):
        put_m(jnp.int32(l), lambda cp: cp.wait())


def experts(n, le, cap, meta, xs, w_gate, w_up, p1, p3):
    width, ffn = w_gate.shape[1:]
    full = n * cap
    hbm = pl.BlockSpec(memory_space=pltpu.HBM)
    vm = pl.BlockSpec(memory_space=pltpu.VMEM)
    dma = pltpu.SemaphoreType.DMA
    return pl.pallas_call(
        functools.partial(experts_kernel, n, le, cap),
        out_shape=(jax.ShapeDtypeStruct((le, full, ffn), BF16), jax.ShapeDtypeStruct(p1.shape, BF16),
                   jax.ShapeDtypeStruct(p3.shape, BF16)),
        in_specs=[pl.BlockSpec(memory_space=pltpu.SMEM), vm, hbm, hbm, vm, vm],
        out_specs=(vm, vm, vm),
        input_output_aliases={4: 1, 5: 2},
        scratch_shapes=[pltpu.VMEM((2, full + TILE, width), BF16), pltpu.VMEM((2, full + cap, ffn), BF16),
                        dma((SLOTS, 2)), dma((2,)), dma((2, n))],
        compiler_params=pltpu.CompilerParams(vmem_limit_bytes=18 * 1024 * 1024),
        name="experts",
    )(meta, xs, w_gate, w_up, p1, p3)[0]


def combine_kernel(n, le, cap, quota, post_ref, qmap_ref, comb_ref, h_ref, ms_ref, w2_ref, out_ref,
                   ring, y_buf, spread, mine, theirs, away, recv_buf, gather0, gather1, w_sem, pair_send, pair_recv,
                   send_sem, recv_sem):
    ep = lax.axis_index("ep")
    chips = n // 2
    x, c = ep // 2, ep % 2
    pa = x * 2 + 1 - c
    bar = pltpu.get_barrier_semaphore()
    for o in range(1, n):
        pl.semaphore_signal(bar, inc=1, device_id={"ep": lax.rem(ep + o, n)}, device_id_type=MESH)

    tokens, width = h_ref.shape
    chunks = width // COLS

    def weights(d, l):
        cols = pl.ds(pl.multiple_of(d * COLS, COLS), COLS)
        return pltpu.make_async_copy(w2_ref.at[l, :, cols], ring.at[lax.rem(d, 2), l], w_sem.at[lax.rem(d, 2), l])

    for d in range(2):
        for l in range(le):
            weights(jnp.int32(d), l).start()

    order = [(2, 0), (2, 1), (1, 0), (3, 0), (1, 1), (3, 1), (0, 1), (0, 0)]
    partner = [order.index((dx, 1 - dc)) for dx, dc in order]
    dests = [lax.rem(x + dx, chips) * 2 + lax.rem(c + dc, 2) for dx, dc in order]
    spot = pl.ds(pl.multiple_of(ep * quota, GRAN), quota)

    row = lax.broadcasted_iota(jnp.int32, (quota, le * cap), 0)
    for k in range(n):
        slots = qmap_ref[pl.ds(dests[k], 1), :]
        spread[k, pl.ds(0, quota), :] = (slots - c * quota == row).astype(F32).astype(BF16)
        spread[k, pl.ds(quota, quota), :] = (slots - (1 - c) * quota == row).astype(F32).astype(BF16)

    def swap(d, k):
        return pltpu.make_async_remote_copy(
            src_ref=away.at[lax.rem(d, 2), k], dst_ref=theirs.at[d, partner[k]], send_sem=pair_send.at[lax.rem(d, 2), k],
            recv_sem=pair_recv.at[d, partner[k]], device_id={"ep": pa}, device_id_type=MESH)

    def push(d, k):
        return pltpu.make_async_remote_copy(
            src_ref=mine.at[d, k], dst_ref=recv_buf.at[d, spot], send_sem=send_sem.at[d, k], recv_sem=recv_sem.at[d, k],
            device_id={"ep": dests[k]}, device_id_type=MESH)

    def send(d):
        for k in range(n):
            swap(d, partner[k]).wait_recv()
            if k == n - 1:
                recv_buf[d, spot, :] = mine[d, k] + theirs[d, k]
            else:
                mine[d, k] = mine[d, k] + theirs[d, k]
                push(d, k).start()

    def project(d, some):
        for l in some:
            weights(d, l).wait()
        for l in some:
            y = jnp.dot(ms_ref[l], ring[lax.rem(d, 2), l], preferred_element_type=F32)
            y_buf[:, pl.ds(l * cap, cap), :] = y.astype(BF16).reshape(n, cap, COLS)

    def chunk(d, carry):
        @pl.when(d > 1)
        def _():
            send(d - 1)

        project(d, range(le // 2, le))

        @pl.when(d + 2 < chunks)
        def _():
            for l in range(le):
                weights(d + 2, l).start()

        @pl.when(d > 1)
        def _():
            for k in range(n):
                swap(d - 2, k).wait_send()

        for k in range(n):
            both = jnp.dot(spread[k], y_buf[dests[k]], preferred_element_type=F32).astype(BF16)
            away[lax.rem(d, 2), k] = both[quota:]
            mine[d, k] = both[:quota]
        for k in range(n):
            swap(d, k).start()

        @pl.when(d == 0)
        def _():
            send(d)

        @pl.when(d + 1 < chunks)
        def _():
            project(d + 1, range(le // 2))

        return carry

    project(jnp.int32(0), range(le // 2))
    pl.semaphore_wait(bar, n - 1)
    lax.fori_loop(0, chunks, chunk, 0)
    send(jnp.int32(chunks - 1))

    def tables(r, carry):
        some = pl.ds(pl.multiple_of(r * 32, 32), 32)
        lane = lax.broadcasted_iota(jnp.int32, (32, n * quota), 1)
        for k, table in enumerate((gather0, gather1)):
            pos = (comb_ref[some, 4 + k:5 + k] * (2 * quota) + comb_ref[some, k:k + 1]).astype(jnp.int32)
            table[some, :] = (lane == pos).astype(F32).astype(BF16)
        return carry

    lax.fori_loop(0, tokens // 32, tables, 0)
    g0, g1 = comb_ref[:, 2:3], comb_ref[:, 3:4]
    alpha, beta = post_ref[0], post_ref[1]

    def finish(d, carry):
        for k in range(n - 1):
            push(d, k).wait_recv()
        cols = pl.ds(pl.multiple_of(d * COLS, COLS), COLS)
        got = recv_buf[d]
        y0 = jnp.dot(gather0[...], got, preferred_element_type=F32)
        y1 = jnp.dot(gather1[...], got, preferred_element_type=F32)
        mixed = g0 * y0 + g1 * y1
        out_ref[:, cols] = (alpha * h_ref[:, cols].astype(F32) + beta * mixed).astype(out_ref.dtype)
        for k in range(n - 1):
            push(d, k).wait_send()
        return carry

    lax.fori_loop(0, chunks, finish, 0)
    for d in range(chunks - 2, chunks):
        for k in range(n):
            swap(jnp.int32(d), k).wait_send()


def combine(n, le, cap, quota, cid, post_scale, qmap, comb, hidden, ms, w_down):
    tokens, width = hidden.shape
    ffn = ms.shape[2]
    vm = pl.BlockSpec(memory_space=pltpu.VMEM)
    sm = pl.BlockSpec(memory_space=pltpu.SMEM)
    dma = pltpu.SemaphoreType.DMA
    chunks = width // COLS
    part = pltpu.VMEM((chunks, n, quota, COLS), BF16)
    table = pltpu.VMEM((tokens, n * quota), BF16)
    return pl.pallas_call(
        functools.partial(combine_kernel, n, le, cap, quota),
        out_shape=jax.ShapeDtypeStruct((tokens, width), hidden.dtype),
        in_specs=[sm, vm, vm, vm, vm, pl.BlockSpec(memory_space=pltpu.HBM)],
        out_specs=vm,
        scratch_shapes=[pltpu.VMEM((2, le, ffn, COLS), BF16), pltpu.VMEM((n, le * cap, COLS), BF16),
                        pltpu.VMEM((n, 2 * quota, le * cap), BF16), part, part,
                        pltpu.VMEM((2, n, quota, COLS), BF16), pltpu.VMEM((chunks, n * quota, COLS), BF16), table, table,
                        dma((2, le)), dma((2, n)), dma((chunks, n)), dma((chunks, n)), dma((chunks, n))],
        compiler_params=pltpu.CompilerParams(collective_id=cid, has_side_effects=True,
                                             vmem_limit_bytes=(36 if quota <= 128 else 49) * 1024 * 1024),
        name="combine%d" % quota,
    )(post_scale, qmap, comb, hidden, ms, w_down)


def solution(mesh):
    n = mesh.shape["ep"]

    def local_step(hidden, router_w, expert_ids, w_gate, w_up, w_down, post_scale):
        tokens, width = hidden.shape
        le = w_gate.shape[0]
        cap = tokens // max(1, (n * le) // 8)
        xs, qmap, meta, comb, p1, p3 = dispatch(n, le, cap, hidden, router_w.T, expert_ids.T, w_gate, w_up)
        ms = experts(n, le, cap, meta, xs, w_gate, w_up, p1, p3)
        quotas = [q for q in (96, 128) if q < le * cap] + [le * cap]
        worst = meta[0, le]
        branch = sum((worst > 2 * q).astype(jnp.int32) for q in quotas[:-1])
        return lax.switch(branch, [functools.partial(combine, n, le, cap, q, 2 + k) for k, q in enumerate(quotas)],
                          post_scale, qmap, comb, hidden, ms, w_down)

    tok = P(("dp", "ep"))
    return jax.shard_map(local_step, mesh=mesh, in_specs=(tok, P(), tok, P("ep"), P("ep"), P("ep"), P()),
                         out_specs=tok, check_vma=False)
```

time: 186 us -> 148 us (0.80)
  Pallas kernels: 176 us -> 145 us
  local copies, waits for them, and re-layouts: 7.76 us -> 1.57 us
    pallas_call x1, Pallas kernels: 51.6 us -> 31.4 us  [experts(): pl.pallas_call(functools.partial(experts_kernel, n, le, cap), out_shape=(...]
    pallas_call x1, Pallas kernels: 78 us -> 70.5 us  [combine(): pl.pallas_call(functools.partial(combine_kernel, n, le, cap, quota), out_...]
    unnamed x13 -> x5, local copies, waits for them, and re-layouts: 6.44 us -> 0.99 us
    pallas_call x1, Pallas kernels: 46.8 us -> 43.3 us  [dispatch(): pl.pallas_call(functools.partial(dispatch_kernel, n, le, cap), out_shape=...]
where the time goes in v2:
time: 148 us
  Pallas kernels  145 us (98%)
  local copies, waits for them, and re-layouts  1.57 us (1%)
    pallas_call x1, Pallas kernels, combine(): pl.pallas_call(functools.partial(combine_kernel, n, le, cap, quota), out_...  70.5 us
    pallas_call x1, Pallas kernels, dispatch(): pl.pallas_call(functools.partial(dispatch_kernel, n, le, cap), out_shape=...  43.3 us
    pallas_call x1, Pallas kernels, experts(): pl.pallas_call(functools.partial(experts_kernel, n, le, cap), out_shape=(...  31.4 us

profile of v2, /device:TPU:81, one launch (start us, length us, event | category | flops | bytes accessed | tf_op | source)
XLA Modules:
  0.0 148.5 jit_solution(10552884760161782401)
XLA Ops:
  0.0 43.3 %dispatch.1 = (bf16[4,8,64,2048]{3,2,1,0:T(8,128)(2,1)S(1)}, s32[8,256]{1,0:T(8,128)S(1)}, s32[8,128]{1,0:T(8,128)S(1)}, f32[256,128]{1,0:T(8,128)S(1)}, bf16[5,...) custom-call(bf16[256,2048]{1,0:T(8,128)(2,1)} %h_hbm.1, f32[32,2048]{1,0:T(8,128)} %bitcast.3, ...), custom_call_target="tpu_custom_call" | custom-call | tf_op jit(solution)/shard_map/dispatch/pallas_call | solution.py:211
  43.3 0.0 copy-start
  43.3 0.0 copy-start.1
  43.3 31.4 %experts.1 = (bf16[4,512,3072]{2,1,0:T(8,128)(2,1)S(1)}, bf16[5,2048,512]{2,1,0:T(8,128)(2,1)S(1)}, bf16[5,2048,512]{2,1,0:T(8,128)(2,1)S(1)}) custom-call(s32[8,128]{1,0:T(8,128)S(1)} %get-tuple-element.70.meta_ref, bf16[4,8,64,2048]{3,2,1,0:T(8,128)(2,1)S(1)} %get-tuple-element.73.xs_ref, ...), custom_call_target="tpu_custom_call", output_to_operand_aliasing={{1}: (4, {}), {2}: (5, {})} | custom-call | tf_op jit(solution)/shard_map/experts/pallas_call | solution.py:335
  74.8 0.6 slice.3
  76.7 0.0 copy-done
  76.7 0.0 copy-done.1
  76.7 70.8 %conditional.1 = (bf16[256,2048]{1,0:T(8,128)(2,1)S(1)}) conditional(s32[]{:T(128)} %bitcast.2, (f32[2]{0:T(128)S(1)}, s32[8,256]{1,0:T(8,128)S(1)}, f32[256,128]{1,0:T(8,128)S(1)}, bf16[256,2048]{1,0:T(8,128)(2,1)S(1)}, bf16[4,512,3072]{2,1,0:T(8,128)(2,1)S(1)}, /*index=5*/bf16[4,3072,2048]{2,1,0:T(8,128)(2,1)}) %tuple.24, ...), branch_computations={%region_0.0_spmd, %region_1.0_spmd, %region_2.0_spmd} | conditional | bytes 8 | solution.py:514
  76.7 70.5 %combine96.1 = bf16[256,2048]{1,0:T(8,128)(2,1)S(1)} custom-call(f32[2]{0:T(128)S(1)} %get-tuple-element.44.post_ref, s32[8,256]{1,0:T(8,128)S(1)} %get-tuple-element.46.qmap_ref, f32[256,128]{1,0:T(8,128)S(1)} %get-tuple-element.47.comb_ref, bf16[256,2048]{1,0:T(8,128)(2,1)S(1)} %get-tuple-element.48.h_ref, ...), custom_call_target="tpu_custom_call" | custom-call | tf_op jit(solution)/shard_map/cond/branch_0_fun/combine96/pallas_call | solution.py:487
  147.5 1.0 copy.19
Async XLA Ops:
  43.3 33.4 %copy-start = (bf16[256,2048]{1,0:T(8,128)(2,1)S(1)}, bf16[256,2048]{1,0:T(8,128)(2,1)}, u32[]{:S(2)}) copy-start(bf16[256,2048]{1,0:T(8,128)(2,1)} %h_hbm.1) | copy-start | bytes 3145732
  43.3 33.4 %copy-start.1 = (f32[2]{0:T(128)S(1)}, f32[2]{0:T(128)}, u32[]{:S(2)}) copy-start(f32[2]{0:T(128)} %param.16) | copy-start | bytes 28
